TPU v7x, 32 devices: a 4x4x1 block of a 4x4x8 slice. The times are simulated.
32 devices in a mesh: rep: 1 (over z), dp: 32 (over x, y, core).
Axes of the slice: x: 4, y: 4, z: 1, core: 2. Of those that a mesh axis runs over, the one named last changes fastest.
The devices are a block of a 4x4x8 slice.
Arguments:
- a: bfloat16 [32, 2, 4096, 896], P(('rep', 'dp'))
- g: bfloat16 [32, 2, 4096, 2560], P(('rep', 'dp'))
Outputs:
- output: bfloat16 [2, 896, 2560], P('rep')
All inputs are finite; a program needn't handle non-finite values.
Results may differ from a plain program's by a relative error of at most 0.012.
Values are sent between devices in bfloat16 or wider.
A program may use at most 768 MiB of HBM per device.

v0:
```python
import jax
import jax.numpy as jnp


def solution(mesh):
    groups = mesh.shape["rep"]

    def step(a, g):
        a, g = (t.reshape(groups, -1, *t.shape[1:]) for t in (a, g))
        sums = jnp.einsum("rsntd,rsntf->rndf", a, g, preferred_element_type=jnp.float32)
        return sums.astype(jnp.bfloat16).reshape(-1, *sums.shape[2:])

    return step
```

profile of v0, /device:TPU:97, one launch (start us, length us, event | category | flops | bytes accessed | tf_op | source)
XLA Modules:
  0.0 188.8 jit_solution(11519034718702115171)
XLA Ops:
  0.0 47.8 %fusion = f32[2,896,2560]{2,1,0:T(8,128)} fusion(bf16[1,2,4096,2560]{3,2,1,0:T(8,128)(2,1)} %param.1, bf16[1,2,4096,896]{3,2,1,0:T(8,128)(2,1)} %param), kind=kOutput, calls=%fused_computation | convolution fusion | flops 37580963840 | bytes 74973184 | tf_op jit(solution)/rsntd,rsntf->rndf/dot_general | solution.py:10
  47.8 141.0 %all-reduce.2 = bf16[2,896,2560]{2,1,0:T(8,128)(2,1)} all-reduce(f32[2,896,2560]{2,1,0:T(8,128)} %fusion), channel_id=1, replica_groups=mesh['axis_0'=32] {'axis_0'}, use_global_device_ids=true, to_apply=%add.clone | all-reduce | flops 4587520 | bytes 27525120 | tf_op jit(solution)/rsntd,rsntf->rndf/dot_general | solution.py:10
where the time goes:
time: 189 us
  blocking collectives  141 us (75%)
  matrix products  47.8 us (25%)
    dot_general x1, blocking collectives, step(): jnp.einsum('rsntd,rsntf->rndf', a, g, preferred_element_type=jnp.float32)  141 us
    dot_general x1, matrix products, step(): jnp.einsum('rsntd,rsntf->rndf', a, g, preferred_element_type=jnp.float32)  47.8 us

commit v1 on v0

v1 whole, which is shorter than its diff:
```python
import math

import jax
import jax.numpy as jnp
from jax import lax
from jax.experimental import pallas as pl
from jax.experimental.pallas import tpu as pltpu
from jax.sharding import PartitionSpec as P

BF, F32 = jnp.bfloat16, jnp.float32
LANES = 128
A_SLOTS, G_SLOTS, P_SLOTS, RING = 4, 3, 12, 4
LAG = (0, 1, 2, 4, 5, 6, 7, 9, 10)


def kernel(side, chunk, a_ref, g_ref, out_ref, araw, at, gbuf, own, d2d_s, d2d_r, r1a_s, r1a_r, r1b_s, r1b_r, r2_s, r2_r,
           asem, gsem, send_sem, recv_sem):
    matrices, tokens, d = a_ref.shape[1:]
    per = g_ref.shape[3] // (2 * LANES)
    blocks = matrices * per
    chunks = tokens // chunk
    leaf = d // side**2

    me = lax.axis_index("dp")
    core = lax.rem(me, 2)
    y = lax.rem(me // 2, side)
    x = me // (2 * side)

    def dev(k, par):
        dx = (lax.rem(x + k + side, side) * side + y) * 2 + core
        dy = (x * side + lax.rem(y + k + side, side)) * 2 + core
        return jnp.where(par == 0, dx, dy)

    partner = me + 1 - 2 * core

    def a_copy(n, i, s):
        return pltpu.make_async_copy(a_ref.at[0, n, pl.ds(i * chunk, chunk), :], araw.at[s], asem.at[s])

    def a_turn(n, i):
        s = lax.rem(i, A_SLOTS)
        a_copy(n, i, s).wait()
        at[lax.rem(n, 2), :, pl.ds(pl.multiple_of(i * chunk, chunk), chunk)] = araw[s].T

    def g_start(b):
        s, n, j = lax.rem(b, G_SLOTS), b // per, lax.rem(b, per)
        for h, cc in ((0, core), (1, 1 - core)):
            col = pl.multiple_of((2 * j + cc) * LANES, LANES)
            pltpu.make_async_copy(
                g_ref.at[0, n, :, pl.ds(col, LANES)], gbuf.at[s, :, pl.ds(h * LANES, LANES)], gsem.at[s]
            ).start()

    def g_wait(b):
        s = lax.rem(b, G_SLOTS)
        pltpu.make_async_copy(gbuf.at[s], gbuf.at[s], gsem.at[s]).wait()

    def send(src, dst, st, b, to):
        pltpu.make_async_remote_copy(
            src_ref=src, dst_ref=dst, send_sem=send_sem.at[st, lax.rem(b, RING)], recv_sem=recv_sem.at[st, b],
            device_id={"dp": to}, device_id_type=pl.DeviceIdType.MESH,
        ).start()

    extent = (d2d_s.at[0], r1a_s.at[0], r1b_s.at[0], r2_s.at[0], r2_s.at[0], (2, side), (2, side // 2), d2d_s.at[0])

    def total(st):
        e = extent[st]
        return d2d_s.at[0, pl.ds(0, e[0] * e[1])] if isinstance(e, tuple) else e

    def wait_sent(st, b):
        pltpu.make_async_copy(total(st), total(st), send_sem.at[st, lax.rem(b, RING)]).wait()

    def wait_got(st, b):
        pltpu.make_async_copy(total(st), total(st), recv_sem.at[st, b]).wait()

    def reuse(st, b):
        @pl.when(b >= RING)
        def _():
            wait_sent(st, b)

    def at_out(b, first, count, cc):
        n, j = b // per, lax.rem(b, per)
        col = pl.multiple_of((2 * j + cc) * LANES, LANES)
        return out_ref.at[n, pl.ds(first, count), :, pl.ds(col, LANES)]

    def place(b):
        par = lax.rem(b, 2)
        return par, jnp.where(par == 0, x, y), jnp.where(par == 0, y, x), lax.rem(b, P_SLOTS), lax.rem(b, RING)

    def s0(b):
        par, pa, pb, s, r = place(b)
        g_wait(b)
        part = jnp.dot(at[lax.rem(b // per, 2)], gbuf[lax.rem(b, G_SLOTS)], preferred_element_type=F32)
        reuse(0, b)
        own[s] = part[:, :LANES].reshape(side, side, leaf, LANES)
        d2d_s[r] = part[:, LANES:].astype(BF).reshape(side**2, leaf, LANES)
        send(d2d_s.at[r], d2d_r.at[b], 0, b, partner)

    def s1(b):
        par, pa, pb, s, r = place(b)
        wait_got(0, b)
        own[s] = own[s] + d2d_r[b].reshape(side, side, leaf, LANES).astype(F32)
        reuse(1, b)
        far = lax.rem(pa + 2, side)
        r1a_s[r] = own[s, far].reshape(2, side // 2, leaf, LANES).astype(BF)
        for i, k in enumerate((1, -1)):
            send(r1a_s.at[r, i], r1a_r.at[b, i], 1, b, dev(k, par))

    def s2(b):
        par, pa, pb, s, r = place(b)
        wait_got(1, b)
        reuse(2, b)
        h = side // 2
        for i, k in enumerate((1, -1)):
            p = lax.rem(pa + k + side, side)
            r1b_s[r, i, pl.ds(i * h, h)] = (own[s, p, pl.ds(i * h, h)] + r1a_r[b, i].astype(F32)).astype(BF)
            r1b_s[r, i, pl.ds((1 - i) * h, h)] = own[s, p, pl.ds((1 - i) * h, h)].astype(BF)
            send(r1b_s.at[r, i], r1b_r.at[b, i], 2, b, dev(k, par))

    def s3(b):
        par, pa, pb, s, r = place(b)
        wait_got(2, b)
        reuse(3, b)
        own[s, pa] = own[s, pa] + r1b_r[b, 0].astype(F32) + r1b_r[b, 1].astype(F32)
        for k in range(1, side):
            r2_s[r, k - 1] = own[s, pa, lax.rem(pb + k, side)].astype(BF)
            send(r2_s.at[r, k - 1], r2_r.at[b, k - 1], 3, b, dev(k, 1 - par))

    def s4(b):
        par, pa, pb, s, r = place(b)
        wait_got(3, b)
        reuse(4, b)
        acc = own[s, pa, pb]
        for k in range(1, side):
            acc = acc + r2_r[b, k - 1].astype(F32)
        mine = at_out(b, pa * side + pb, 1, core)
        mine[...] = acc.astype(BF)[None]
        for k in range(1, side):
            send(mine, mine, 4, b, dev(k, 1 - par))

    def s5(b):
        par, pa, pb, s, r = place(b)
        wait_got(4, b)
        reuse(5, b)
        mine = at_out(b, pa * side, side, core)
        for k in (1, -1):
            send(mine, mine, 5, b, dev(k, par))

    def s6(b):
        par, pa, pb, s, r = place(b)
        wait_got(5, b)
        reuse(6, b)
        h = side // 2
        for i, k in enumerate((1, -1)):
            theirs = at_out(b, lax.rem(pa - k + side, side) * side + i * h, h, core)
            send(theirs, theirs, 6, b, dev(k, par))

    def s7(b):
        wait_got(6, b)
        reuse(7, b)
        half = at_out(b, 0, side**2, core)
        send(half, half, 7, b, partner)

    def s8(b):
        wait_got(7, b)

    g_start(0)
    for i in range(A_SLOTS):
        a_copy(0, i, i).start()
    g_start(1)
    peers = [partner] + [dev(k, par) for par in (0, 1) for k in range(1, side)]
    barrier = pltpu.get_barrier_semaphore()
    for p in peers:
        pl.semaphore_signal(barrier, inc=1, device_id={"dp": p}, device_id_type=pl.DeviceIdType.MESH)

    def first(i, _):
        a_turn(0, i)

        @pl.when(i + A_SLOTS < chunks)
        def _():
            a_copy(0, i + A_SLOTS, lax.rem(i, A_SLOTS)).start()

        return 0

    lax.fori_loop(0, chunks, first, 0)
    pl.semaphore_wait(barrier, len(peers))

    def tick(t, _):
        n, j = t // per, lax.rem(t, per)

        @pl.when((n + 1 < matrices) & (j < chunks))
        def _():
            a_copy(n + 1, j, lax.rem(j, A_SLOTS)).start()

        @pl.when(t + 2 < blocks)
        def _():
            g_start(t + 2)

        @pl.when(t < blocks)
        def _():
            s0(t)

        @pl.when((n + 1 < matrices) & (j >= 1) & (j <= chunks))
        def _():
            a_turn(n + 1, j - 1)

        for st, lag in reversed(list(enumerate((s1, s2, s3, s4, s5, s6, s7, s8), 1))):
            b = t - LAG[st]

            @pl.when((b >= 0) & (b < blocks))
            def _():
                lag(b)

        return 0

    lax.fori_loop(0, blocks + LAG[-1], tick, 0)

    def drain(b, _):
        for st in range(8):
            wait_sent(st, b)
        return 0

    lax.fori_loop(blocks - RING, blocks, drain, 0)


def solution(mesh):
    side = math.isqrt(mesh.shape["dp"] // 2)

    def step(a, g):
        matrices, tokens, d = a.shape[1:]
        f = g.shape[3]
        leaf, blocks = d // side**2, matrices * f // (2 * LANES)
        chunk = tokens // 8
        quarter, h = (side, leaf, LANES), side // 2
        out = pl.pallas_call(
            lambda *refs: kernel(side, chunk, *refs),
            out_shape=OUT((matrices, side**2, leaf, f), BF),
            in_specs=[pl.BlockSpec(memory_space=pl.ANY)] * 2,
            out_specs=pl.BlockSpec(memory_space=OUT_SPACE),
            scratch_shapes=[
                pltpu.VMEM((A_SLOTS, chunk, d), BF),
                pltpu.VMEM((2, d, tokens), BF),
                pltpu.VMEM((G_SLOTS, tokens, 2 * LANES), BF),
                pltpu.VMEM((P_SLOTS, side, *quarter), F32),
                pltpu.VMEM((RING, side**2, leaf, LANES), BF),
                pltpu.VMEM((blocks, side**2, leaf, LANES), BF),
                pltpu.VMEM((RING, 2, h, leaf, LANES), BF),
                pltpu.VMEM((blocks, 2, h, leaf, LANES), BF),
                pltpu.VMEM((RING, 2, *quarter), BF),
                pltpu.VMEM((blocks, 2, *quarter), BF),
                pltpu.VMEM((RING, side - 1, leaf, LANES), BF),
                pltpu.VMEM((blocks, side - 1, leaf, LANES), BF),
                pltpu.SemaphoreType.DMA((A_SLOTS,)),
                pltpu.SemaphoreType.DMA((G_SLOTS,)),
                pltpu.SemaphoreType.DMA((8, RING)),
                pltpu.SemaphoreType.DMA((8, blocks)),
            ],
            compiler_params=pltpu.CompilerParams(
                collective_id=0, has_side_effects=True, vmem_limit_bytes=50 * 2**20
            ),
            name="sums",
        )(a, g)
        return out.reshape(matrices, d, f)

    spec = P(("rep", "dp"))
    return jax.shard_map(step, mesh=mesh, in_specs=(spec, spec), out_specs=P("rep"), check_vma=False)


OUT, OUT_SPACE = pltpu.VMEM, pltpu.VMEM
```

time: 189 us -> 130 us (0.69)
  blocking collectives: 141 us -> 0 us
  Pallas kernels: 0 us -> 126 us
  matrix products: 47.8 us -> 0 us
  local copies, waits for them, and re-layouts: 0 us -> 3.66 us
    dot_general x1 -> x0, blocking collectives: 141 us -> none  [step(): jnp.einsum('rsntd,rsntf->rndf', a, g, preferred_element_type=jnp.float32)]
    pallas_call x0 -> x1, Pallas kernels: none -> 126 us  [step(): pl.pallas_call(lambda *refs: kernel(side, chunk, *refs), out_shape=OUT((m...]
    dot_general x1 -> x0, matrix products: 47.8 us -> none  [step(): jnp.einsum('rsntd,rsntf->rndf', a, g, preferred_element_type=jnp.float32)]
    unnamed x0 -> x1, local copies, waits for them, and re-layouts: none -> 3.66 us
where the time goes in v1:
time: 130 us
  Pallas kernels  126 us (97%)
  local copies, waits for them, and re-layouts  3.66 us (3%)
    pallas_call x1, Pallas kernels, step(): pl.pallas_call(lambda *refs: kernel(side, chunk, *refs), out_shape=OUT((m...  126 us
    unnamed x1, local copies, waits for them, and re-layouts  3.66 us

profile of v1, /device:TPU:97, one launch (start us, length us, event | category | flops | bytes accessed | tf_op | source)
XLA Modules:
  0.0 129.8 jit_solution(2556826106436253110)
XLA Ops:
  0.0 126.1 %sums.1 = bf16[2,16,56,2560]{3,2,1,0:T(8,128)(2,1)S(1)} custom-call(bf16[1,2,4096,896]{3,2,1,0:T(8,128)(2,1)} %refs_0_.1, bf16[1,2,4096,2560]{3,2,1,0:T(8,128)(2,1)} %refs_1_.1), custom_call_target="tpu_custom_call" | custom-call | tf_op jit(solution)/shard_map/sums/pallas_call | solution.py:233
  126.1 3.7 %copy.4 = bf16[2,896,2560]{2,1,0:T(8,128)(2,1)} copy(bf16[2,896,2560]{2,1,0:T(8,128)(2,1)S(1)} %bitcast.1) | data formatting | bytes 18350080

commit v2 on v1

v2 whole, which is shorter than its diff:
```python
import math

import jax
import jax.numpy as jnp
from jax import lax
from jax.experimental import pallas as pl
from jax.experimental.pallas import tpu as pltpu
from jax.sharding import PartitionSpec as P

BF, F32 = jnp.bfloat16, jnp.float32
LANES = 128
G_SLOTS, RING = 3, 8
LAG = (0, 1, 3, 6, 8, 10, 13, 15, 16)
FAST = 6
FLAG = (0, 1, 4, 6, 8, 11, 12)
P_SLOTS = max(LAG[4], FLAG[3]) + 1
STAGES = 10


def kernel(side, chunk, a_ref, g_ref, out_ref, araw, at0, at1, gbuf, own, d2d_s, d2d_r, r1a_s, r1a_r, r1b_s, r1b_r, r2a_s, r2a_r, r2b_s, r2b_r,
           asem, gsem, send_sem, recv_sem):
    matrices, tokens, d = a_ref.shape[1:]
    per = g_ref.shape[3] // (2 * LANES)
    blocks = matrices * per
    chunks = tokens // chunk
    leaf = d // side**2

    me = lax.axis_index("dp")
    core = lax.rem(me, 2)
    y = lax.rem(me // 2, side)
    x = me // (2 * side)

    def dev(k, par):
        dx = (lax.rem(x + k + side, side) * side + y) * 2 + core
        dy = (x * side + lax.rem(y + k + side, side)) * 2 + core
        return jnp.where(par == 0, dx, dy)

    partner = me + 1 - 2 * core

    def a_copy(n, i):
        return pltpu.make_async_copy(a_ref.at[0, n, pl.ds(i * chunk, chunk), :], araw.at[i], asem.at[i])

    at = (at0, at1)

    def a_turn(n, i):
        at[n % 2][:, pl.ds(pl.multiple_of(i * chunk, chunk), chunk)] = araw[i].T

    def split(b):
        n = sum((b >= k * per).astype(jnp.int32) for k in range(1, matrices)) + jnp.int32(0)
        return n, b - n * per

    def g_start(b):
        s = lax.rem(b, G_SLOTS)
        n, j = split(b)
        for h, cc in ((0, core), (1, 1 - core)):
            col = pl.multiple_of((2 * j + cc) * LANES, LANES)
            pltpu.make_async_copy(
                g_ref.at[0, n, :, pl.ds(col, LANES)], gbuf.at[s, :, pl.ds(h * LANES, LANES)], gsem.at[s]
            ).start()

    def g_wait(b):
        s = lax.rem(b, G_SLOTS)
        pltpu.make_async_copy(gbuf.at[s], gbuf.at[s], gsem.at[s]).wait()

    def send(src, dst, st, b, to):
        pltpu.make_async_remote_copy(
            src_ref=src, dst_ref=dst, send_sem=send_sem.at[st, lax.rem(b, RING)], recv_sem=recv_sem.at[st, b],
            device_id={"dp": to}, device_id_type=pl.DeviceIdType.MESH,
        ).start()

    extent = (
        d2d_s.at[0], r1a_s.at[0], r1b_s.at[0], r2a_s.at[0], r2b_s.at[0], r2b_s.at[0], r2a_s.at[0],
        (2, side), (2, side // 2), d2d_s.at[0],
    )

    def total(st):
        e = extent[st]
        return d2d_s.at[0, pl.ds(0, e[0] * e[1])] if isinstance(e, tuple) else e

    def wait_sent(st, b):
        pltpu.make_async_copy(total(st), total(st), send_sem.at[st, lax.rem(b, RING)]).wait()

    def wait_got(st, b):
        pltpu.make_async_copy(total(st), total(st), recv_sem.at[st, b]).wait()

    def reuse(st, b):
        @pl.when(b >= RING)
        def _():
            wait_sent(st, b)

    def at_out(b, first, count, cc):
        n, j = split(b)
        col = pl.multiple_of((2 * j + cc) * LANES, LANES)
        return out_ref.at[n, pl.ds(first, count), :, pl.ds(col, LANES)]

    def place(b):
        par = lax.rem(b, 2)
        return par, jnp.where(par == 0, x, y), jnp.where(par == 0, y, x), lax.rem(b, P_SLOTS), lax.rem(b, RING)

    peers = [partner] + [dev(k, par) for par in (0, 1) for k in range(1, side)]
    barrier = pltpu.get_barrier_semaphore()

    def s0(n, b, turn):
        par, pa, pb, s, r = place(b)
        j = split(b)[1]
        g_wait(b)
        if turn:
            a_copy(n + 1, j - 1).wait()
        reuse(0, b)
        part = jnp.dot(at[n % 2][...], gbuf[lax.rem(b, G_SLOTS)], preferred_element_type=F32)
        if turn:
            a_turn(n + 1, j - 1)
        own[s] = part[:, :LANES].reshape(side, side, leaf, LANES)
        d2d_s[r] = part[:, LANES:].astype(BF).reshape(side**2, leaf, LANES)
        if n == 0:

            @pl.when(b == 0)
            def _():
                pl.semaphore_wait(barrier, len(peers))

        send(d2d_s.at[r], d2d_r.at[b], 0, b, partner)

    def s1(b):
        par, pa, pb, s, r = place(b)
        wait_got(0, b)
        own[s] = own[s] + d2d_r[b].reshape(side, side, leaf, LANES).astype(F32)
        reuse(1, b)
        far = lax.rem(pa + 2, side)
        r1a_s[r] = own[s, far].reshape(2, side // 2, leaf, LANES).astype(BF)
        for i, k in enumerate((1, -1)):
            send(r1a_s.at[r, i], r1a_r.at[b, i], 1, b, dev(k, par))

    def s2(b):
        par, pa, pb, s, r = place(b)
        wait_got(1, b)
        reuse(2, b)
        h = side // 2
        for i, k in enumerate((1, -1)):
            p = lax.rem(pa + k + side, side)
            r1b_s[r, i, pl.ds(i * h, h)] = (own[s, p, pl.ds(i * h, h)] + r1a_r[b, i].astype(F32)).astype(BF)
            r1b_s[r, i, pl.ds((1 - i) * h, h)] = own[s, p, pl.ds((1 - i) * h, h)].astype(BF)
            send(r1b_s.at[r, i], r1b_r.at[b, i], 2, b, dev(k, par))

    def s3(b):
        par, pa, pb, s, r = place(b)
        wait_got(2, b)
        own[s, pa] = own[s, pa] + r1b_r[b, 0].astype(F32) + r1b_r[b, 1].astype(F32)
        leaves(b)

    def leaves(b):
        par, pa, pb, s, r = place(b)
        reuse(3, b)
        reuse(4, b)
        r2a_s[r, 0] = own[s, pa, lax.rem(pb + 2, side)].astype(BF)
        send(r2a_s.at[r, 0], r2a_r.at[b, 0], 3, b, dev(2, 1 - par))
        for i, k in enumerate((1, -1)):
            r2b_s[r, i] = own[s, pa, lax.rem(pb + k + side, side)].astype(BF)
            send(r2b_s.at[r, i], r2b_r.at[b, i], 4, b, dev(k, 1 - par))

    def s4(b):
        par, pa, pb, s, r = place(b)
        wait_got(3, b)
        wait_got(4, b)
        reuse(5, b)
        reuse(6, b)
        mine = at_out(b, pa * side + pb, 1, core)
        got = r2b_r[b, 0].astype(F32) + r2b_r[b, 1].astype(F32) + r2a_r[b, 0].astype(F32)
        mine[...] = (own[s, pa, pb] + got).astype(BF)[None]
        send(mine, mine, 6, b, dev(2, 1 - par))
        for k in (1, -1):
            send(mine, mine, 5, b, dev(k, 1 - par))

    def s5(b):
        par, pa, pb, s, r = place(b)
        wait_got(5, b)
        wait_got(6, b)
        reuse(7, b)
        mine = at_out(b, pa * side, side, core)
        for k in (1, -1):
            send(mine, mine, 7, b, dev(k, par))

    def s6(b):
        par, pa, pb, s, r = place(b)
        wait_got(7, b)
        reuse(8, b)
        h = side // 2
        for i, k in enumerate((1, -1)):
            theirs = at_out(b, lax.rem(pa - k + side, side) * side + i * h, h, core)
            send(theirs, theirs, 8, b, dev(k, par))

    def s7(b):
        wait_got(8, b)
        reuse(9, b)
        half = at_out(b, 0, side**2, core)
        send(half, half, 9, b, partner)

    def s8(b):
        wait_got(9, b)

    def f1(b):
        par, pa, pb, s, r = place(b)
        wait_got(0, b)
        own[s] = own[s] + d2d_r[b].reshape(side, side, leaf, LANES).astype(F32)
        reuse(1, b)
        reuse(2, b)
        r1a_s[r] = own[s, lax.rem(pa + 2, side)].reshape(2, side // 2, leaf, LANES).astype(BF)
        send(r1a_s.at[r], r1a_r.at[b], 1, b, dev(2, par))
        for i, k in enumerate((1, -1)):
            r1b_s[r, i] = own[s, lax.rem(pa + k + side, side)].astype(BF)
            send(r1b_s.at[r, i], r1b_r.at[b, i], 2, b, dev(k, par))

    def f2(b):
        par, pa, pb, s, r = place(b)
        wait_got(1, b)
        wait_got(2, b)
        got = r1a_r[b].reshape(side, leaf, LANES).astype(F32)
        own[s, pa] = own[s, pa] + r1b_r[b, 0].astype(F32) + r1b_r[b, 1].astype(F32) + got
        leaves(b)

    def f4(b):
        par, pa, pb, s, r = place(b)
        wait_got(5, b)
        wait_got(6, b)
        reuse(7, b)
        reuse(8, b)
        mine = at_out(b, pa * side, side, core)
        send(mine, mine, 8, b, dev(2, par))
        for k in (1, -1):
            send(mine, mine, 7, b, dev(k, par))

    def f5(b):
        wait_got(7, b)
        s7(b)

    g_start(jnp.int32(0))
    for i in range(chunks):
        a_copy(0, i).start()
    g_start(jnp.int32(1))
    for p in peers:
        pl.semaphore_signal(barrier, inc=1, device_id={"dp": p}, device_id_type=pl.DeviceIdType.MESH)

    def first(i, _):
        a_copy(0, i).wait()
        a_turn(0, i)
        return 0

    lax.fori_loop(0, chunks, first, 0)

    def later(t):
        for st, stage in reversed(list(enumerate((s1, s2, s3, s4, s5, s6, s7, s8), 1))):
            b = t - LAG[st]

            @pl.when((b >= 0) & (b < blocks - FAST))
            def _():
                stage(b)

        for st, stage in reversed(list(enumerate((f1, f2, s4, f4, f5, s8), 1))):
            b = t - FLAG[st]

            @pl.when((b >= blocks - FAST) & (b < blocks))
            def _():
                stage(b)

    for n in range(matrices):
        turns = n + 1 < matrices

        def tick(t, _):
            j = t - n * per
            if turns:

                @pl.when(j < chunks)
                def _():
                    a_copy(n + 1, j).start()

            @pl.when(t + 2 < blocks)
            def _():
                g_start(t + 2)

            if turns:
                busy = (j >= 1) & (j <= chunks)

                @pl.when(busy)
                def _():
                    s0(n, t, True)

                @pl.when(jnp.logical_not(busy))
                def _():
                    s0(n, t, False)
            else:
                s0(n, t, False)
            later(t)
            return 0

        lax.fori_loop(n * per, (n + 1) * per, tick, 0)

    def tail(t, _):
        later(t)
        return 0

    lax.fori_loop(blocks, blocks + max(LAG[-1] - FAST, FLAG[-1]), tail, 0)

    def drain(b, _):
        for st in range(STAGES):
            wait_sent(st, b)
        return 0

    lax.fori_loop(blocks - RING, blocks, drain, 0)


def solution(mesh):
    side = math.isqrt(mesh.shape["dp"] // 2)

    def step(a, g):
        matrices, tokens, d = a.shape[1:]
        f = g.shape[3]
        leaf, blocks = d // side**2, matrices * f // (2 * LANES)
        chunk = tokens // 8
        quarter, h = (side, leaf, LANES), side // 2
        out = pl.pallas_call(
            lambda *refs: kernel(side, chunk, *refs),
            out_shape=OUT((matrices, side**2, leaf, f), BF),
            in_specs=[pl.BlockSpec(memory_space=pl.ANY)] * 2,
            out_specs=pl.BlockSpec(memory_space=OUT_SPACE),
            scratch_shapes=[
                pltpu.VMEM((8, chunk, d), BF),
                pltpu.VMEM((d, tokens), BF),
                pltpu.VMEM((d, tokens), BF),
                pltpu.VMEM((G_SLOTS, tokens, 2 * LANES), BF),
                pltpu.VMEM((P_SLOTS, side, *quarter), F32),
                pltpu.VMEM((RING, side**2, leaf, LANES), BF),
                pltpu.VMEM((blocks, side**2, leaf, LANES), BF),
                pltpu.VMEM((RING, 2, h, leaf, LANES), BF),
                pltpu.VMEM((blocks, 2, h, leaf, LANES), BF),
                pltpu.VMEM((RING, 2, *quarter), BF),
                pltpu.VMEM((blocks, 2, *quarter), BF),
                pltpu.VMEM((RING, 1, leaf, LANES), BF),
                pltpu.VMEM((blocks, 1, leaf, LANES), BF),
                pltpu.VMEM((RING, 2, leaf, LANES), BF),
                pltpu.VMEM((blocks, 2, leaf, LANES), BF),
                pltpu.SemaphoreType.DMA((8,)),
                pltpu.SemaphoreType.DMA((G_SLOTS,)),
                pltpu.SemaphoreType.DMA((STAGES, RING)),
                pltpu.SemaphoreType.DMA((STAGES, blocks)),
            ],
            compiler_params=pltpu.CompilerParams(
                collective_id=0, has_side_effects=True, vmem_limit_bytes=53 * 2**20
            ),
            name="sums",
        )(a, g)
        return out.reshape(matrices, d, f)

    spec = P(("rep", "dp"))
    return jax.shard_map(step, mesh=mesh, in_specs=(spec, spec), out_specs=P("rep"), check_vma=False)


OUT, OUT_SPACE = pltpu.VMEM, pltpu.VMEM
```

time: 130 us -> 95.7 us (0.74)
  Pallas kernels: 126 us -> 91.9 us
    pallas_call x1, Pallas kernels: 126 us -> 91.9 us  [step(): pl.pallas_call(lambda *refs: kernel(side, chunk, *refs), out_shape=OUT((m...]
where the time goes in v2:
time: 95.7 us; the launch traced here: 95.6 us
  Pallas kernels  91.9 us (96%)
  local copies, waits for them, and re-layouts  3.66 us (4%)
    pallas_call x1, Pallas kernels, step(): pl.pallas_call(lambda *refs: kernel(side, chunk, *refs), out_shape=OUT((m...  91.9 us
    unnamed x1, local copies, waits for them, and re-layouts  3.66 us

profile of v2, /device:TPU:97, one launch (start us, length us, event | category | flops | bytes accessed | tf_op | source)
XLA Modules:
  0.0 95.6 jit_solution(16002518363655934707)
XLA Ops:
  0.0 91.9 %sums.1 = bf16[2,16,56,2560]{3,2,1,0:T(8,128)(2,1)S(1)} custom-call(bf16[1,2,4096,896]{3,2,1,0:T(8,128)(2,1)} %refs_0_.1, bf16[1,2,4096,2560]{3,2,1,0:T(8,128)(2,1)} %refs_1_.1), custom_call_target="tpu_custom_call" | custom-call | tf_op jit(solution)/shard_map/sums/pallas_call | solution.py:319
  92.0 3.7 %copy.4 = bf16[2,896,2560]{2,1,0:T(8,128)(2,1)} copy(bf16[2,896,2560]{2,1,0:T(8,128)(2,1)S(1)} %bitcast.1) | data formatting | bytes 18350080
